TPU v7x, 8 devices: a whole 2x2x1 slice. The times are simulated.
8 devices in a mesh: dp: 1 (over z), ch: 2 (over y), wd: 4 (over x, core).
Axes of the slice: x: 2, y: 2, z: 1, core: 2. Of those that a mesh axis runs over, the one named last changes fastest.
Arguments:
- resid_in: bfloat16 [16384, 2048], P('dp', 'wd')
- seg_pos: int32 [4, 4096], P('dp')
- gain_temporal: bfloat16 [2048], P('wd')
- w_x: bfloat16 [2048, 2560], P('wd', 'ch')
- bias_x: bfloat16 [2560], P('ch')
- w_y: bfloat16 [2048, 2560], P('wd', 'ch')
- bias_y: bfloat16 [2560], P('ch')
- conv_w: bfloat16 [4, 2560], P(None, 'ch')
- conv_bias: bfloat16 [2560], P('ch')
- lam_param: float32 [2560], P('ch')
- rgate_w: bfloat16 [10, 256, 256], P('ch')
- rgate_b: bfloat16 [2560], P('ch')
- igate_w: bfloat16 [10, 256, 256], P('ch')
- igate_b: bfloat16 [2560], P('ch')
- w_o: bfloat16 [2560, 2048], P('ch', 'wd')
- bias_o: bfloat16 [2048], P('wd')
- gain_mlp: bfloat16 [2048], P('wd')
- w_g: bfloat16 [2048, 6144], P('wd', 'ch')
- bias_g: bfloat16 [6144], P('ch')
- w_u: bfloat16 [2048, 6144], P('wd', 'ch')
- bias_u: bfloat16 [6144], P('ch')
- w_d: bfloat16 [6144, 2048], P('ch', 'wd')
- bias_d: bfloat16 [2048], P('wd')
Outputs:
- output: bfloat16 [16384, 2048], P('dp', 'wd')
All inputs are finite; a program needn't handle non-finite values.
Results may differ from a plain program's by a relative error of at most 0.0129377.
Values are sent between devices in bfloat16 or wider.
A program may use at most 1 GiB of HBM per device.

v0:
```python
import jax
import jax.numpy as jnp
from jax import lax
from jax.experimental import pallas as pl
from jax.experimental.pallas import tpu as pltpu
from jax.sharding import PartitionSpec as P

MESH = pl.DeviceIdType.MESH
F32, BF16 = jnp.float32, jnp.bfloat16
EPS = 1e-6
LANES = 256
CHUNK = 256
UP = 512
NX = 4
NWD, NCH = 4, 2
NDEV = NWD * NCH
ANY = pl.BlockSpec(memory_space=pl.ANY)
VMEM_LIMIT = 62 * 1024 * 1024
OWN_X, OWN_Y, OWN_P, X_P, X_Y, Y_P, Y_X, D_P = range(8)


def gelu(v):
    return 0.5 * v * (1.0 + jnp.tanh(0.7978845608028654 * (v + 0.044715 * (v * v * v))))


def sigmoid(v):
    return 1.0 / (1.0 + jnp.exp(-v))


def shuffle_matrix(transposed):
    rows = lax.broadcasted_iota(jnp.int32, (CHUNK, CHUNK), 0)
    cols = lax.broadcasted_iota(jnp.int32, (CHUNK, CHUNK), 1)
    out, src = (cols, rows) if transposed else (rows, cols)
    return jnp.where((out % 8) * (CHUNK // 8) + out // 8 == src, 1.0, 0.0).astype(BF16)


def layer(resid, pos_ref, w_y, w_x, w_o, w_g, w_u, w_d, rgate, igate, vch, vmlp, vwd,
          out, g_y, g_x, g_o, g_g, g_u, g_d, x_far,
          n_s, acc_s, t_a, t_b, t_c, rg_s, ig_s, par_s, mlp_s, vwd_s, x_s, raw_s, u_s, h_s, prod_s, y_s, tail_s, h0_s, act_s,
          msg_out, msg_in, ssem, rsem, tsem, xssem, xrsem, pssem, prsem, lsem, mssem, mrsem, xlsem, ossem, orsem, fssem, frsem, olsem):
    ch, wd = lax.axis_index("ch"), lax.axis_index("wd")
    core = lax.rem(wd, 2)
    me = ch * NWD + wd
    wx, wp = lax.rem(wd + 2, NWD), wd + 1 - 2 * core
    dev_x, dev_y, dev_p = (0, ch, wx), (0, 1 - ch, wd), (0, ch, wp)
    id_x, id_y, id_d = ch * NWD + wx, (1 - ch) * NWD + wd, (1 - ch) * NWD + wx
    tokens, model = n_s.shape
    width = resid.shape[1]
    blocks = w_y.shape[1] // LANES
    halves = blocks * NCH
    groups = w_g.shape[1] // LANES
    steps = tokens // CHUNK
    ups = tokens // UP
    every = slice(None)

    def remote(src, dst, device, send, recv):
        return pltpu.make_async_remote_copy(src_ref=src, dst_ref=dst, send_sem=send, recv_sem=recv, device_id=device,
                                            device_id_type=MESH)

    def cols_of(i):
        return pl.ds(pl.multiple_of(i * LANES, LANES), LANES)

    def first(i):
        return [(w_y, g_y, every, cols_of(i)), (w_x, g_x, every, cols_of(i)), (w_o, g_o, i, every)]

    def second(i):
        return [(w_g, g_g, every, cols_of(i)), (w_u, g_u, every, cols_of(i)), (w_d, g_d, i, every)]

    def cut(unit, owner, part):
        own, far, rows, cols = unit
        if rows == every:
            size, base = own.shape[0], 0
        else:
            size, base = LANES, rows * LANES
        if part is not None:
            size = size // 2
            base = base + part * size
        rows = pl.ds(pl.multiple_of(base, size) if not isinstance(base, int) else base, size)
        return own.at[rows, cols] if owner is None else far.at[owner, rows, cols]

    def transfer(kind, g, u, unit, split):
        owner, part, device = {OWN_X: (None, None, dev_x), OWN_Y: (None, None, dev_y), OWN_P: (None, None, dev_p),
                               X_P: (id_x, None, dev_p), X_Y: (id_x, 0 if split else None, dev_y),
                               Y_P: (id_y, None, dev_p), Y_X: (id_y, 1, dev_x), D_P: (id_d, None, dev_p)}[kind]
        src = cut(unit, owner, part)
        dst = cut(unit, me if owner is None else owner, part)
        return remote(src, dst, device, ssem.at[kind, g, u], rsem.at[kind, g, u])

    def send(g, units, kinds, split):
        for kind in kinds:
            for u, unit in enumerate(units):
                transfer(kind, g, u, unit, split).start()

    def forward(g, units, split):
        for u, unit in enumerate(units):
            transfer(OWN_X, g, u, unit, split).wait_recv()
            transfer(X_Y, g, u, unit, split).start()
            transfer(X_P, g, u, unit, split).start()
        for u, unit in enumerate(units):
            transfer(OWN_Y, g, u, unit, split).wait_recv()
            if split:
                transfer(Y_X, g, u, unit, split).start()
            transfer(Y_P, g, u, unit, split).start()

    def relay(g, units, split):
        for u, unit in enumerate(units):
            transfer(X_Y, g, u, unit, split).wait_recv()
            if split:
                transfer(Y_X, g, u, unit, split).wait_recv()
            transfer(D_P, g, u, unit, split).start()

    def ready(g, units, split):
        for u, unit in enumerate(units):
            for kind in (OWN_P, X_P, Y_P, D_P):
                transfer(kind, g, u, unit, split).wait_recv()

    def drain(g, units, split):
        for u, unit in enumerate(units):
            for kind in range(8):
                if split or kind != Y_X:
                    transfer(kind, g, u, unit, split).wait_send()

    both = (OWN_X, OWN_Y, OWN_P)

    def tile(units, owner, slot, place, own, start):
        for u, (unit, buf) in enumerate(zip(units, (t_a, t_b, t_c))):
            d = pltpu.make_async_copy(cut(unit, None if own else owner, None), buf.at[slot, place], tsem.at[slot, u, place])
            if start:
                d.start()
            else:
                d.wait()

    def load_tiles(units, slot, count, base):
        @pl.loop(0, count)
        def _(k):
            owner = base + k

            @pl.when(owner == me)
            def _():
                tile(units, owner, slot, k, True, True)

            @pl.when(owner != me)
            def _():
                tile(units, owner, slot, k, False, True)

    def wait_tiles(units, slot, count):
        @pl.loop(0, count)
        def _(k):
            tile(units, 0, slot, k, False, False)

    send(0, first(0), both, False)
    small = [(vch, par_s.at[pl.ds(ch * blocks, blocks)]), (rgate, rg_s.at[pl.ds(ch * blocks, blocks)]),
             (igate, ig_s.at[pl.ds(ch * blocks, blocks)]), (vmlp, mlp_s.at[ch])]
    small_sends = [remote(s, d, dev_y, pssem.at[i], prsem.at[i]) for i, (s, d) in enumerate(small)]
    for p in (1, 2, 3):
        i = len(small) + p - 1
        small_sends.append(remote(vwd, vwd_s.at[wd], (0, ch, lax.rem(wd + p, NWD)), pssem.at[i], prsem.at[i]))
    small_own = [pltpu.make_async_copy(s, d, lsem.at[i]) for i, (s, d) in enumerate(small + [(vwd, vwd_s.at[wd])])]
    for d in small_sends + small_own:
        d.start()

    rows_x = tokens // NX

    def x_copy(p, q):
        peer = lax.rem(wd + p, NWD)
        return remote(resid.at[pl.ds((ch * NWD + peer) * tokens + q * rows_x, rows_x)],
                      x_far.at[pl.ds(q * rows_x, rows_x), pl.ds(pl.multiple_of(wd * width, width), width)],
                      (0, ch, peer), xssem.at[p - 1, q], xrsem.at[p - 1, q])

    for q in range(NX):
        for p in (2, 1, 3):
            x_copy(p, q).start()
    for g in range(1, blocks):
        send(g, first(g), (OWN_X,), False)
    forward(0, first(0), False)
    for g in range(1, blocks):
        send(g, first(g), (OWN_Y, OWN_P), False)
    for d in small_own:
        d.wait()
    for d in small_sends:
        d.wait()
    relay(0, first(0), False)
    ready(0, first(0), False)
    load_tiles(first(0), 0, NWD, 0)

    def wide(i):
        return jnp.concatenate([vwd_s[k, i:i + 1, :] for k in range(NWD)], axis=1)

    def x_load(c):
        rows = pl.ds(c * CHUNK, CHUNK)
        for k in range(NWD):
            cols = pl.ds(k * width, width)

            @pl.when(wd == k)
            def _():
                pltpu.make_async_copy(resid.at[pl.ds(me * tokens + c * CHUNK, CHUNK)], x_s.at[:, cols], xlsem.at[k]).start()

            @pl.when(wd != k)
            def _():
                pltpu.make_async_copy(x_far.at[rows, cols], x_s.at[:, cols], xlsem.at[k]).start()

        for k in range(NWD):
            cols = pl.ds(k * width, width)
            pltpu.make_async_copy(x_far.at[rows, cols], x_s.at[:, cols], xlsem.at[k]).wait()

    mix = shuffle_matrix(False)

    @pl.loop(0, steps)
    def _(c):
        @pl.when(lax.rem(c, steps // NX) == 0)
        def _():
            for p in (1, 2, 3):
                x_copy(p, c // (steps // NX)).wait_recv()

        x_load(c)
        rows = pl.ds(c * CHUNK, CHUNK)
        vals = jnp.dot(mix, x_s[...], preferred_element_type=F32)
        scale = lax.rsqrt(jnp.mean(vals * vals, axis=1, keepdims=True) + EPS)
        n_s[rows, :] = (vals * scale * (1.0 + wide(0))).astype(BF16)
        acc_s[rows, :] = vals + wide(1)

    def message(i):
        return remote(msg_out.at[i], msg_in.at[i], dev_p, mssem.at[i], mrsem.at[i])

    def project(q, slot, tiles):
        vals = n_s[pl.ds(q * CHUNK, CHUNK), :]
        raw_s[slot, 0] = jnp.dot(vals, t_a[tiles, 0:NWD].reshape(model, LANES), preferred_element_type=F32)
        raw_s[slot, 1] = jnp.dot(vals, t_b[tiles, 0:NWD].reshape(model, LANES), preferred_element_type=F32)

    def recur(q, slot, tiles, block):
        def row(i):
            return par_s[block, i:i + 1, :]

        rows = pl.ds(q * CHUNK, CHUNK)
        time = CHUNK // 8
        pos = pos_ref[rows, :]
        pos = jnp.concatenate([pos] * (LANES // pos.shape[1]), axis=1)
        y_s[...] = gelu(raw_s[slot, 0] + row(1)).astype(BF16)
        u = (raw_s[slot, 1] + row(0)).astype(BF16).astype(F32)
        u_s[24:, :] = u
        sub = lax.broadcasted_iota(jnp.int32, (8, LANES), 0)
        last = u[CHUNK - 24:, :]
        for k in range(3):
            edge = jnp.where(sub == 7, tail_s[k * 8:(k + 1) * 8, :], last[k * 8:(k + 1) * 8, :])
            u_s[k * 8:(k + 1) * 8, :] = pltpu.roll(edge, 1, 0)
        tail_s[...] = last
        c = row(2) + u * row(3)
        for k in range(1, 4):
            c = c + jnp.where(pos >= k, u_s[pl.ds(24 - 8 * k, CHUNK), :], 0.0) * row(3 + k)
        c16 = c.astype(BF16)
        rate = sigmoid(jnp.dot(c16, rg_s[block], preferred_element_type=F32) + row(8))
        inflow = sigmoid(jnp.dot(c16, ig_s[block], preferred_element_type=F32) + row(9))
        log_a = rate * row(7)
        a = jnp.exp(log_a)
        scale = jnp.sqrt(jnp.tanh(-log_a) * (1.0 + a * a))
        reset = pos == 0
        a = jnp.where(reset, 0.0, a)
        scale = jnp.where(reset, 1.0, scale)
        b = scale * inflow * c16.astype(F32)
        h, prod = b[0:8, :], a[0:8, :]
        h_s[0:8, :] = h
        prod_s[0:8, :] = prod
        for t in range(1, time):
            at = a[t * 8:(t + 1) * 8, :]
            h = at * h + b[t * 8:(t + 1) * 8, :]
            prod = at * prod
            h_s[t * 8:(t + 1) * 8, :] = h
            prod_s[t * 8:(t + 1) * 8, :] = prod
        for k in (1, 2, 4):
            far = sub >= k
            h = jnp.where(far, h + prod * pltpu.roll(h, k, 0), h)
            prod = jnp.where(far, prod * pltpu.roll(prod, k, 0), prod)
        before = h0_s[...]
        ends = h + prod * before
        carry = jnp.where(sub == 0, before, pltpu.roll(ends, 1, 0))
        h0_s[...] = jnp.broadcast_to(ends[7:8, :], (8, LANES))
        hid = h_s[...].reshape(time, 8, LANES) + prod_s[...].reshape(time, 8, LANES) * carry[None]
        mixed = (hid.reshape(CHUNK, LANES) * y_s[...].astype(F32)).astype(BF16)
        for k in range(NWD):
            cols = pl.ds(k * width, width)
            acc_s[rows, cols] += jnp.dot(mixed, t_c[tiles, k], preferred_element_type=F32)

    @pl.loop(0, halves)
    def _(i):
        jj, side = i // 2, lax.rem(i, 2)
        tiles = side
        block = side * blocks + jj

        for g in range(1, blocks):
            @pl.when(i == g)
            def _(g=g):
                forward(g, first(g), False)

        for at, b in ((3, 0), (4, 1), (5, 2), (7, 3)):
            @pl.when(i == at)
            def _(b=b):
                send(blocks + b, second(b), both, True)

        for at, b in ((6, 0), (8, 1)):
            @pl.when(i == at)
            def _(b=b):
                forward(blocks + b, second(b), True)

        def relay_next(of):
            for g in range(1, blocks):
                @pl.when((core == of) & (i == 2 * g - 1))
                def _(g=g):
                    relay(g, first(g), False)

            @pl.when((core == of) & (i == halves - 1))
            def _():
                relay(blocks, second(0), True)

        relay_next(1)
        wait_tiles(first(0), tiles, NWD)
        project(0, 0, tiles)

        @pl.when(core == 0)
        def _():
            h0_s[...] = jnp.zeros_like(h0_s)
            tail_s[...] = jnp.zeros_like(tail_s)

        @pl.when(core == 1)
        def _():
            message(i).wait_recv()
            tail_s[...] = msg_in[i, 0:24, :]
            h0_s[...] = msg_in[i, 24:32, :]

        @pl.loop(0, steps - 1)
        def _(q):
            @pl.when((q == 3) & (side == 0))
            def _():
                load_tiles(first(jj), 1, NWD, NWD)

            slot = lax.rem(q, 2)
            project(q + 1, 1 - slot, tiles)
            recur(q, slot, tiles, block)

        recur(steps - 1, (steps - 1) % 2, tiles, block)

        @pl.when(core == 0)
        def _():
            msg_out[i, 0:24, :] = tail_s[...]
            msg_out[i, 24:32, :] = h0_s[...]
            message(i).start()

        relay_next(0)

        @pl.when((side == 1) & (i < halves - 1))
        def _():
            for g in range(1, blocks):
                @pl.when(jj == g - 1)
                def _(g=g):
                    ready(g, first(g), False)
            load_tiles(first(jj + 1), 0, NWD, 0)

    ready(blocks, second(0), True)
    load_tiles(second(0), 0, NDEV, 0)

    @pl.loop(0, steps)
    def _(c):
        rows = pl.ds(c * CHUNK, CHUNK)
        vals = acc_s[rows, :]
        scale = lax.rsqrt(jnp.mean(vals * vals, axis=1, keepdims=True) + EPS)
        n_s[rows, :] = (vals * scale * (1.0 + wide(2))).astype(BF16)
        acc_s[rows, :] = vals + wide(3)

    def rows_of(i):
        return pl.ds(i * UP, UP)

    def up(i, slot, tiles, b):
        vals = n_s[rows_of(i), :]
        for c in range(NCH):
            part = slice(c * NWD, (c + 1) * NWD)
            gate = jnp.dot(vals, t_a[tiles, part].reshape(model, LANES), preferred_element_type=F32) + mlp_s[c, 0:1, cols_of(b)]
            upper = jnp.dot(vals, t_b[tiles, part].reshape(model, LANES), preferred_element_type=F32) + mlp_s[c, 1:2, cols_of(b)]
            act_s[slot, :, c * LANES:(c + 1) * LANES] = (gelu(gate) * upper).astype(BF16)

    def down(i, slot, tiles):
        for k in range(NWD):
            cols = pl.ds(k * width, width)
            more = [jnp.dot(act_s[slot, :, c * LANES:(c + 1) * LANES], t_c[tiles, c * NWD + k], preferred_element_type=F32) for c in range(NCH)]
            acc_s[rows_of(i), cols] += more[0] + more[1]

    base = me * tokens
    own_cols = pl.ds(pl.multiple_of(wd * width, width), width)

    def direct(p, i):
        peer = lax.rem(wd + p, NWD)
        return remote(n_s.at[rows_of(i), pl.ds(pl.multiple_of(peer * width, width), width)], out.at[pl.ds(base + i * UP, UP)],
                      (0, ch, peer), ossem.at[p - 1, i], orsem.at[p - 1, i])

    def across(i):
        return remote(n_s.at[rows_of(i), own_cols], out.at[pl.ds(base + i * UP, UP)], dev_y, fssem.at[0, i], frsem.at[0, i])

    def onward(p, i):
        came = lax.rem(wd + NWD - p, NWD)
        here = pl.ds((ch * NWD + came) * tokens + i * UP, UP)
        return remote(out.at[here], out.at[here], dev_y, fssem.at[p, i], frsem.at[p, i])

    def keep(i):
        return pltpu.make_async_copy(n_s.at[rows_of(i), own_cols], out.at[pl.ds(base + i * UP, UP)], olsem.at[i])

    def hand_out(i):
        back = shuffle_matrix(True)
        for c in range(UP // CHUNK):
            rows = pl.ds(i * UP + c * CHUNK, CHUNK)
            n_s[rows, :] = jnp.dot(back, acc_s[rows, :].astype(BF16), preferred_element_type=F32).astype(BF16)
        across(i).start()
        for p in (2, 1, 3):
            direct(p, i).start()
        keep(i).start()

    def ahead(s):
        return s + 2 - (s + 7) // 12

    @pl.loop(0, groups)
    def _(s):
        tiles = lax.rem(s, 2)

        @pl.when(s + 4 < groups)
        def _():
            send(blocks + s + 4, second(s + 4), both, True)

        @pl.when((ahead(s + 1) > ahead(s)) & (ahead(s) < groups))
        def _():
            forward(blocks + ahead(s), second(ahead(s)), True)

        wait_tiles(second(0), tiles, NDEV)
        up(0, 0, tiles, s)

        @pl.loop(1, ups)
        def _(i):
            @pl.when((i == 2) & (s + 1 < groups))
            def _():
                relay(blocks + s + 1, second(s + 1), True)
                ready(blocks + s + 1, second(s + 1), True)
                load_tiles(second(s + 1), 1 - tiles, NDEV, 0)

            slot = lax.rem(i, 2)
            up(i, slot, tiles, s)
            down(i - 1, 1 - slot, tiles)

            @pl.when(s == groups - 1)
            def _():
                hand_out(i - 1)

        down(ups - 1, (ups - 1) % 2, tiles)

    hand_out(ups - 1)

    for i in range(ups):
        for p in (1, 2, 3):
            direct(p, i).wait_recv()
            onward(p, i).start()
    for g in range(blocks):
        drain(g, first(g), False)

    @pl.loop(0, groups)
    def _(b):
        drain(blocks + b, second(b), True)

    for q in range(NX):
        for p in (1, 2, 3):
            x_copy(p, q).wait_send()

    @pl.when(core == 0)
    def _():
        @pl.loop(0, halves)
        def _(i):
            message(i).wait_send()

    for i in range(ups):
        keep(i).wait()
        across(i).wait()
        for p in (1, 2, 3):
            direct(p, i).wait_send()
            onward(p, i).wait()


def solution(mesh):
    row_spec = P("dp", "wd")
    specs = (row_spec, P("dp", None), P("wd"), P("wd", "ch"), P("ch"), P("wd", "ch"), P("ch"), P(None, "ch"), P("ch"), P("ch"), P("ch", None, None), P("ch"), P("ch", None, None), P("ch"), P("ch", "wd"), P("wd"), P("wd"), P("wd", "ch"), P("ch"), P("wd", "ch"), P("ch"), P("ch", "wd"), P("wd"))

    def local_layer(resid_in, seg_pos, gain_temporal, w_x, bias_x, w_y, bias_y, conv_w, conv_bias, lam_param, rgate_w, rgate_b, igate_w, igate_b, w_o, bias_o, gain_mlp, w_g, bias_g, w_u, bias_u, w_d, bias_d):
        tokens, width = resid_in.shape
        model = width * NWD
        rows = tokens // NDEV
        blocks = w_x.shape[1] // LANES
        groups = w_g.shape[1] // LANES
        total = NCH * blocks
        ch, wd = lax.axis_index("ch"), lax.axis_index("wd")
        per_chan = jnp.stack([bias_x, bias_y, conv_bias, *conv_w, -8.0 * jax.nn.softplus(-lam_param), rgate_b, igate_b]).astype(F32)
        per_chan = jnp.pad(per_chan, ((0, 16 - per_chan.shape[0]), (0, 0)))
        vch = per_chan.reshape(16, blocks, LANES).transpose(1, 0, 2)
        vmlp = jnp.pad(jnp.stack([bias_g, bias_u]).astype(F32), ((0, 6), (0, 0)))
        vwd = jnp.pad(jnp.stack([gain_temporal, bias_o, gain_mlp, bias_d]).astype(F32), ((0, 4), (0, 0)))
        pos = lax.dynamic_index_in_dim(seg_pos.reshape(NDEV, rows), ch * NWD + wd, 0, keepdims=False)
        pos = pos.reshape(rows // CHUNK, 8, CHUNK // 8).transpose(0, 2, 1).reshape(rows, 1)
        pos = jnp.broadcast_to(pos, (rows, 128))

        def like(w):
            return jax.ShapeDtypeStruct((NDEV, *w.shape), BF16)

        dma = pltpu.SemaphoreType.DMA
        ups = rows // UP
        kinds = (8, blocks + groups, 3)
        outs = pl.pallas_call(
            layer,
            out_shape=[jax.ShapeDtypeStruct((tokens, width), BF16), like(w_y), like(w_x), like(w_o), like(w_g), like(w_u), like(w_d),
                       jax.ShapeDtypeStruct((rows, model), BF16)],
            in_specs=[ANY, pl.BlockSpec(memory_space=pltpu.VMEM)] + [ANY] * 11,
            out_specs=[ANY] * 8,
            scratch_shapes=[pltpu.VMEM((rows, model), BF16), pltpu.VMEM((rows, model), F32),
                            pltpu.VMEM((2, NDEV, width, LANES), BF16), pltpu.VMEM((2, NDEV, width, LANES), BF16),
                            pltpu.VMEM((2, NDEV, LANES, width), BF16),
                            pltpu.VMEM((total, LANES, LANES), BF16), pltpu.VMEM((total, LANES, LANES), BF16),
                            pltpu.VMEM((total, 16, LANES), F32), pltpu.VMEM((NCH, *vmlp.shape), F32), pltpu.VMEM((NWD, *vwd.shape), F32),
                            pltpu.VMEM((CHUNK, model), BF16), pltpu.VMEM((2, 2, CHUNK, LANES), F32), pltpu.VMEM((CHUNK + 24, LANES), F32),
                            pltpu.VMEM((CHUNK, LANES), F32), pltpu.VMEM((CHUNK, LANES), F32), pltpu.VMEM((CHUNK, LANES), BF16),
                            pltpu.VMEM((24, LANES), F32), pltpu.VMEM((8, LANES), F32), pltpu.VMEM((2, UP, NCH * LANES), BF16),
                            pltpu.VMEM((total, 32, LANES), F32), pltpu.VMEM((total, 32, LANES), F32),
                            dma(kinds), dma(kinds), dma((2, 3, NDEV)), dma((3, NX)), dma((3, NX)), dma((7,)), dma((7,)), dma((5,)),
                            dma((total,)), dma((total,)), dma((NWD,)), dma((3, ups)), dma((3, ups)), dma((4, ups)), dma((4, ups)), dma((ups,))],
            compiler_params=pltpu.CompilerParams(has_side_effects=True, vmem_limit_bytes=VMEM_LIMIT),
            name="layer",
        )(resid_in, pos, w_y, w_x, w_o, w_g, w_u, w_d, rgate_w, igate_w, vch, vmlp, vwd)
        return outs[0]

    return jax.shard_map(local_layer, mesh=mesh, in_specs=specs, out_specs=row_spec, check_vma=False)
```

profile of v0, /device:TPU:0, one launch (start us, length us, event | category | flops | bytes accessed | tf_op | source)
XLA Modules:
  0.0 811.8 jit_solution(15611893329231459307)
XLA Ops:
  0.0 0.7 stack.79
  0.7 0.7 stack.80
  1.4 0.7 stack.81
  2.0 0.7 stack.82
  2.7 0.7 reshape.15
  3.4 0.7 reshape.16
  4.1 0.7 reshape.17
  4.8 0.7 reshape.18
  5.5 0.7 reshape.19
  6.2 0.6 fusion.11.vwd
  6.8 0.7 fusion.12
  7.5 0.7 stack.76
  8.2 0.7 stack.77
  8.9 0.9 slice_convert_fusion
  9.8 0.1 stack.75
  9.9 0.6 copy.29
  10.6 0.9 reshape.12
  11.5 0.1 reshape.13
  11.5 0.7 fusion.3.vmlp
  12.2 0.1 copy.25
  12.3 0.1 broadcast_in_dim.7
  12.4 1.3 broadcast_in_dim.8.pos_ref
  13.7 784.2 %layer.1 = (bf16[16384,512]{1,0:T(8,128)(2,1)}, bf16[8,512,1280]{2,1,0:T(8,128)(2,1)}, bf16[8,512,1280]{2,1,0:T(8,128)(2,1)}, bf16[8,1280,512]{2,1,0:T(8,128)(2,...) custom-call(bf16[16384,512]{1,0:T(8,128)(2,1)} %resid.1, ...), custom_call_target="tpu_custom_call" | custom-call | tf_op jit(solution)/shard_map/layer/pallas_call | solution.py:508
  798.0 13.8 %copy.31 = bf16[16384,512]{1,0:T(8,128)(2,1)} copy(bf16[16384,512]{1,0:T(8,128)(2,1)} %get-tuple-element.6) | data formatting | bytes 33554432
  (3 shorter events, 0.0 us)
where the time goes:
time: 813 us; the launch traced here: 812 us
  Pallas kernels  784 us (96%)
  local copies, waits for them, and re-layouts  24.6 us (3%)
    pallas_call x1, Pallas kernels, local_layer(): pl.pallas_call(layer, out_shape=[jax.ShapeDtypeStruct((tokens, width), BF...  784 us

commit v1 on v0

--- a/solution.py
+++ b/solution.py
@@ -11,11 +11,12 @@
 LANES = 256
 CHUNK = 256
 UP = 512
+DOWN = 2
 NX = 4
 NWD, NCH = 4, 2
 NDEV = NWD * NCH
 ANY = pl.BlockSpec(memory_space=pl.ANY)
-VMEM_LIMIT = 62 * 1024 * 1024
+VMEM_LIMIT = 65_800_000
 OWN_X, OWN_Y, OWN_P, X_P, X_Y, Y_P, Y_X, D_P = range(8)
 
 
@@ -36,8 +37,8 @@
 
 def layer(resid, pos_ref, w_y, w_x, w_o, w_g, w_u, w_d, rgate, igate, vch, vmlp, vwd,
           out, g_y, g_x, g_o, g_g, g_u, g_d, x_far,
-          n_s, acc_s, t_a, t_b, t_c, rg_s, ig_s, par_s, mlp_s, vwd_s, x_s, raw_s, u_s, h_s, prod_s, y_s, tail_s, h0_s, act_s,
-          msg_out, msg_in, ssem, rsem, tsem, xssem, xrsem, pssem, prsem, lsem, mssem, mrsem, xlsem, ossem, orsem, fssem, frsem, olsem):
+          n_s, acc_s, act_s, t_w, par_s, mlp_s, vwd_s, raw_s, u_s, h_s, prod_s, y_s, tail_s, h0_s,
+          msg_out, msg_in, ssem, rsem, dssem, drsem, tsem, xssem, xrsem, pssem, prsem, lsem, mssem, mrsem, xlsem, ossem, orsem, fssem, frsem, olsem):
     ch, wd = lax.axis_index("ch"), lax.axis_index("wd")
     core = lax.rem(wd, 2)
     me = ch * NWD + wd
@@ -52,6 +53,17 @@
     steps = tokens // CHUNK
     ups = tokens // UP
     every = slice(None)
+    deep = w_d.shape[0] // DOWN
+
+    x_s = act_s.at[1, pl.ds(2 * LANES, CHUNK), pl.ds(0, model)]
+    gate_rows = 3 * LANES
+
+    def gate_area(which, side):
+        cols = pl.ds(pl.multiple_of((2 * which + side) * LANES, LANES), LANES)
+        return act_s.at[1, pl.ds(gate_rows, blocks * LANES), cols]
+
+    def back_tile(slot, k):
+        return act_s.at[1, pl.ds(pl.multiple_of(slot * LANES, LANES), LANES), pl.ds(pl.multiple_of(k * width, width), width)]
 
     def remote(src, dst, device, send, recv):
         return pltpu.make_async_remote_copy(src_ref=src, dst_ref=dst, send_sem=send, recv_sem=recv, device_id=device,
@@ -64,7 +76,7 @@
         return [(w_y, g_y, every, cols_of(i)), (w_x, g_x, every, cols_of(i)), (w_o, g_o, i, every)]
 
     def second(i):
-        return [(w_g, g_g, every, cols_of(i)), (w_u, g_u, every, cols_of(i)), (w_d, g_d, i, every)]
+        return [(w_g, g_g, every, cols_of(i)), (w_u, g_u, every, cols_of(i))]
 
     def cut(unit, owner, part):
         own, far, rows, cols = unit
@@ -122,9 +134,24 @@
 
     both = (OWN_X, OWN_Y, OWN_P)
 
+    def down_piece(kind, d):
+        owner, device = {OWN_X: (None, dev_x), OWN_Y: (None, dev_y), OWN_P: (None, dev_p), X_P: (id_x, dev_p),
+                         Y_P: (id_y, dev_p), Y_X: (id_y, dev_x), D_P: (id_d, dev_p)}[kind]
+        rows = pl.ds(d * deep, deep)
+        src = w_d.at[rows] if owner is None else g_d.at[owner, rows]
+        return remote(src, g_d.at[me if owner is None else owner, rows], device, dssem.at[kind, d], drsem.at[kind, d])
+
+    def forward_down(d):
+        down_piece(OWN_Y, d).wait_recv()
+        down_piece(Y_X, d).start()
+        down_piece(Y_P, d).start()
+        down_piece(OWN_X, d).wait_recv()
+        down_piece(X_P, d).start()
+
     def tile(units, owner, slot, place, own, start):
-        for u, (unit, buf) in enumerate(zip(units, (t_a, t_b, t_c))):
-            d = pltpu.make_async_copy(cut(unit, None if own else owner, None), buf.at[slot, place], tsem.at[slot, u, place])
+        for u, unit in enumerate(units):
+            buf = back_tile(slot, place) if u == 2 else t_w.at[2 * u + slot, place]
+            d = pltpu.make_async_copy(cut(unit, None if own else owner, None), buf, tsem.at[slot, u, place])
             if start:
                 d.start()
             else:
@@ -149,14 +176,13 @@
             tile(units, 0, slot, k, False, False)
 
     send(0, first(0), both, False)
-    small = [(vch, par_s.at[pl.ds(ch * blocks, blocks)]), (rgate, rg_s.at[pl.ds(ch * blocks, blocks)]),
-             (igate, ig_s.at[pl.ds(ch * blocks, blocks)]), (vmlp, mlp_s.at[ch])]
+    small = [(vch, par_s.at[pl.ds(ch * blocks, blocks)]), (rgate, gate_area(0, ch)), (igate, gate_area(1, ch)), (vmlp, mlp_s.at[ch])]
     small_sends = [remote(s, d, dev_y, pssem.at[i], prsem.at[i]) for i, (s, d) in enumerate(small)]
     for p in (1, 2, 3):
         i = len(small) + p - 1
         small_sends.append(remote(vwd, vwd_s.at[wd], (0, ch, lax.rem(wd + p, NWD)), pssem.at[i], prsem.at[i]))
     small_own = [pltpu.make_async_copy(s, d, lsem.at[i]) for i, (s, d) in enumerate(small + [(vwd, vwd_s.at[wd])])]
-    for d in small_sends + small_own:
+    for d in small_sends[:1] + small_sends[3:] + small_own:
         d.start()
 
     rows_x = tokens // NX
@@ -175,9 +201,10 @@
     forward(0, first(0), False)
     for g in range(1, blocks):
         send(g, first(g), (OWN_Y, OWN_P), False)
-    for d in small_own:
-        d.wait()
-    for d in small_sends:
+        if g == 1:
+            for d in small_sends[1:3]:
+                d.start()
+    for d in small_own + small_sends[4:]:
         d.wait()
     relay(0, first(0), False)
     ready(0, first(0), False)
@@ -219,13 +246,16 @@
         n_s[rows, :] = (vals * scale * (1.0 + wide(0))).astype(BF16)
         acc_s[rows, :] = vals + wide(1)
 
+    for d in small_sends[:4]:
+        d.wait()
+
     def message(i):
         return remote(msg_out.at[i], msg_in.at[i], dev_p, mssem.at[i], mrsem.at[i])
 
     def project(q, slot, tiles):
         vals = n_s[pl.ds(q * CHUNK, CHUNK), :]
-        raw_s[slot, 0] = jnp.dot(vals, t_a[tiles, 0:NWD].reshape(model, LANES), preferred_element_type=F32)
-        raw_s[slot, 1] = jnp.dot(vals, t_b[tiles, 0:NWD].reshape(model, LANES), preferred_element_type=F32)
+        raw_s[slot, 0] = jnp.dot(vals, t_w[tiles, 0:NWD].reshape(model, LANES), preferred_element_type=F32)
+        raw_s[slot, 1] = jnp.dot(vals, t_w[2 + tiles, 0:NWD].reshape(model, LANES), preferred_element_type=F32)
 
     def recur(q, slot, tiles, block):
         def row(i):
@@ -248,8 +278,9 @@
         for k in range(1, 4):
             c = c + jnp.where(pos >= k, u_s[pl.ds(24 - 8 * k, CHUNK), :], 0.0) * row(3 + k)
         c16 = c.astype(BF16)
-        rate = sigmoid(jnp.dot(c16, rg_s[block], preferred_element_type=F32) + row(8))
-        inflow = sigmoid(jnp.dot(c16, ig_s[block], preferred_element_type=F32) + row(9))
+        gates = [gate_area(which, block // blocks)[pl.ds(pl.multiple_of(lax.rem(block, blocks) * LANES, LANES), LANES), :] for which in range(2)]
+        rate = sigmoid(jnp.dot(c16, gates[0], preferred_element_type=F32) + row(8))
+        inflow = sigmoid(jnp.dot(c16, gates[1], preferred_element_type=F32) + row(9))
         log_a = rate * row(7)
         a = jnp.exp(log_a)
         scale = jnp.sqrt(jnp.tanh(-log_a) * (1.0 + a * a))
@@ -278,7 +309,19 @@
         mixed = (hid.reshape(CHUNK, LANES) * y_s[...].astype(F32)).astype(BF16)
         for k in range(NWD):
             cols = pl.ds(k * width, width)
-            acc_s[rows, cols] += jnp.dot(mixed, t_c[tiles, k], preferred_element_type=F32)
+            acc_s[rows, cols] += jnp.dot(mixed, back_tile(tiles, k)[...], preferred_element_type=F32)
+
+    def came(i):
+        return jnp.maximum(i - 4, 0)
+
+    def pass_on(low, high):
+        @pl.loop(low, high)
+        def _(b):
+            forward(blocks + b, second(b), True)
+
+            @pl.when(b + 3 < groups)
+            def _():
+                send(blocks + b + 3, second(b + 3), both, True)
 
     @pl.loop(0, halves)
     def _(i):
@@ -291,15 +334,11 @@
             def _(g=g):
                 forward(g, first(g), False)
 
-        for at, b in ((3, 0), (4, 1), (5, 2), (7, 3)):
-            @pl.when(i == at)
-            def _(b=b):
-                send(blocks + b, second(b), both, True)
-
-        for at, b in ((6, 0), (8, 1)):
-            @pl.when(i == at)
-            def _(b=b):
-                forward(blocks + b, second(b), True)
+        @pl.when((i >= 2) & (i < 5))
+        def _():
+            send(blocks + i - 2, second(i - 2), both, True)
+
+        pass_on(came(i), came(i + 1))
 
         def relay_next(of):
             for g in range(1, blocks):
@@ -354,6 +393,7 @@
                     ready(g, first(g), False)
             load_tiles(first(jj + 1), 0, NWD, 0)
 
+    pass_on(6, 7)
     ready(blocks, second(0), True)
     load_tiles(second(0), 0, NDEV, 0)
 
@@ -368,97 +408,167 @@
     def rows_of(i):
         return pl.ds(i * UP, UP)
 
-    def up(i, slot, tiles, b):
+    def up(i, tiles, b):
         vals = n_s[rows_of(i), :]
         for c in range(NCH):
             part = slice(c * NWD, (c + 1) * NWD)
-            gate = jnp.dot(vals, t_a[tiles, part].reshape(model, LANES), preferred_element_type=F32) + mlp_s[c, 0:1, cols_of(b)]
-            upper = jnp.dot(vals, t_b[tiles, part].reshape(model, LANES), preferred_element_type=F32) + mlp_s[c, 1:2, cols_of(b)]
-            act_s[slot, :, c * LANES:(c + 1) * LANES] = (gelu(gate) * upper).astype(BF16)
-
-    def down(i, slot, tiles):
-        for k in range(NWD):
-            cols = pl.ds(k * width, width)
-            more = [jnp.dot(act_s[slot, :, c * LANES:(c + 1) * LANES], t_c[tiles, c * NWD + k], preferred_element_type=F32) for c in range(NCH)]
-            acc_s[rows_of(i), cols] += more[0] + more[1]
+            gate = jnp.dot(vals, t_w[tiles, part].reshape(model, LANES), preferred_element_type=F32) + mlp_s[c, 0:1, cols_of(b)]
+            upper = jnp.dot(vals, t_w[2 + tiles, part].reshape(model, LANES), preferred_element_type=F32) + mlp_s[c, 1:2, cols_of(b)]
+            act_s[c, rows_of(i), cols_of(b)] = (gelu(gate) * upper).astype(BF16)
+
+    def ahead(s):
+        return jnp.minimum(s + 7 - s // 5, groups)
+
+    @pl.loop(0, groups)
+    def _(s):
+        tiles = lax.rem(s, 2)
+        pass_on(ahead(s), ahead(s + 1))
+
+        @pl.when(s == 2)
+        def _():
+            for d in range(DOWN):
+                for kind in both:
+                    down_piece(kind, d).start()
+
+        @pl.when(s == 9)
+        def _():
+            forward_down(0)
+
+        wait_tiles(second(0), tiles, NDEV)
+
+        @pl.loop(0, ups)
+        def _(i):
+            @pl.when((i == 2) & (s + 1 < groups))
+            def _():
+                relay(blocks + s + 1, second(s + 1), True)
+                ready(blocks + s + 1, second(s + 1), True)
+                load_tiles(second(s + 1), 1 - tiles, NDEV, 0)
+
+            up(i, tiles, s)
+
+    forward_down(1)
 
     base = me * tokens
-    own_cols = pl.ds(pl.multiple_of(wd * width, width), width)
-
-    def direct(p, i):
-        peer = lax.rem(wd + p, NWD)
-        return remote(n_s.at[rows_of(i), pl.ds(pl.multiple_of(peer * width, width), width)], out.at[pl.ds(base + i * UP, UP)],
-                      (0, ch, peer), ossem.at[p - 1, i], orsem.at[p - 1, i])
+
+    def col_block(b):
+        return lax.rem(wd + lax.rem(b, 2) * (1 - 2 * core) + 2 * (b // 2) + NWD, NWD)
+
+    def wide_cols(b):
+        return pl.ds(pl.multiple_of(col_block(b) * width, width), width)
 
     def across(i):
-        return remote(n_s.at[rows_of(i), own_cols], out.at[pl.ds(base + i * UP, UP)], dev_y, fssem.at[0, i], frsem.at[0, i])
-
-    def onward(p, i):
-        came = lax.rem(wd + NWD - p, NWD)
-        here = pl.ds((ch * NWD + came) * tokens + i * UP, UP)
-        return remote(out.at[here], out.at[here], dev_y, fssem.at[p, i], frsem.at[p, i])
+        return remote(n_s.at[rows_of(i), wide_cols(0)], out.at[pl.ds(base + i * UP, UP)], dev_y, fssem.at[0, i], frsem.at[0, i])
 
     def keep(i):
-        return pltpu.make_async_copy(n_s.at[rows_of(i), own_cols], out.at[pl.ds(base + i * UP, UP)], olsem.at[i])
-
-    def hand_out(i):
+        return pltpu.make_async_copy(n_s.at[rows_of(i), wide_cols(0)], out.at[pl.ds(base + i * UP, UP)], olsem.at[i])
+
+    def direct(b, i):
+        return remote(n_s.at[rows_of(i), wide_cols(b)], out.at[pl.ds(base + i * UP, UP)], (0, ch, col_block(b)),
+                      ossem.at[b - 1, i], orsem.at[b - 1, i])
+
+    def onward(b, i):
+        here = pl.ds((ch * NWD + col_block(b)) * tokens + i * UP, UP)
+        return remote(out.at[here], out.at[here], dev_y, fssem.at[b, i], frsem.at[b, i])
+
+    def load_down(b, p):
+        side = lax.rem(ch + p // DOWN, NCH)
+        owner = side * NWD + col_block(b)
+        third = deep // width
+
+        @pl.loop(0, 2 * third)
+        def _(e):
+            rows = pl.ds(pl.multiple_of(lax.rem(p, DOWN) * deep + lax.rem(e, third) * width, width), width)
+            cols = cols_of(e // third)
+
+            @pl.when(owner == me)
+            def _():
+                pltpu.make_async_copy(w_d.at[rows, cols], t_w.at[p, e], tsem.at[p, 2, e]).start()
+
+            @pl.when(owner != me)
+            def _():
+                pltpu.make_async_copy(g_d.at[owner, rows, cols], t_w.at[p, e], tsem.at[p, 2, e]).start()
+
+    def wait_down(p):
+        @pl.loop(0, 2 * (deep // width))
+        def _(e):
+            pltpu.make_async_copy(w_d.at[pl.ds(0, width), cols_of(0)], t_w.at[p, e], tsem.at[p, 2, e]).wait()
+
+    def down(b, p, i):
+        third = deep // width
+        side = lax.rem(ch + p // DOWN, NCH)
+        vals = act_s[side, rows_of(i), pl.ds(pl.multiple_of(lax.rem(p, DOWN) * deep, deep), deep)]
+        for half in range(2):
+            cols = pl.ds(pl.multiple_of(col_block(b) * width + half * LANES, LANES), LANES)
+            acc_s[rows_of(i), cols] += jnp.dot(vals, t_w[p, half * third:(half + 1) * third].reshape(deep, LANES), preferred_element_type=F32)
+
+    def hand_out(b, i):
         back = shuffle_matrix(True)
         for c in range(UP // CHUNK):
             rows = pl.ds(i * UP + c * CHUNK, CHUNK)
-            n_s[rows, :] = jnp.dot(back, acc_s[rows, :].astype(BF16), preferred_element_type=F32).astype(BF16)
-        across(i).start()
-        for p in (2, 1, 3):
-            direct(p, i).start()
-        keep(i).start()
-
-    def ahead(s):
-        return s + 2 - (s + 7) // 12
-
-    @pl.loop(0, groups)
-    def _(s):
-        tiles = lax.rem(s, 2)
-
-        @pl.when(s + 4 < groups)
-        def _():
-            send(blocks + s + 4, second(s + 4), both, True)
-
-        @pl.when((ahead(s + 1) > ahead(s)) & (ahead(s) < groups))
-        def _():
-            forward(blocks + ahead(s), second(ahead(s)), True)
-
-        wait_tiles(second(0), tiles, NDEV)
-        up(0, 0, tiles, s)
-
-        @pl.loop(1, ups)
-        def _(i):
-            @pl.when((i == 2) & (s + 1 < groups))
-            def _():
-                relay(blocks + s + 1, second(s + 1), True)
-                ready(blocks + s + 1, second(s + 1), True)
-                load_tiles(second(s + 1), 1 - tiles, NDEV, 0)
-
-            slot = lax.rem(i, 2)
-            up(i, slot, tiles, s)
-            down(i - 1, 1 - slot, tiles)
-
-            @pl.when(s == groups - 1)
-            def _():
-                hand_out(i - 1)
-
-        down(ups - 1, (ups - 1) % 2, tiles)
-
-    hand_out(ups - 1)
-
-    for i in range(ups):
-        for p in (1, 2, 3):
-            direct(p, i).wait_recv()
-            onward(p, i).start()
+            n_s[rows, wide_cols(b)] = jnp.dot(back, acc_s[rows, wide_cols(b)].astype(BF16), preferred_element_type=F32).astype(BF16)
+
+        @pl.when(b == 0)
+        def _():
+            across(i).start()
+            keep(i).start()
+
+        @pl.when(b > 0)
+        def _():
+            direct(b, i).start()
+
+    @pl.loop(0, NWD)
+    def _(b):
+        @pl.when(b == 1)
+        def _():
+            for d in range(DOWN):
+                down_piece(OWN_P, d).wait_recv()
+                down_piece(Y_P, d).wait_recv()
+
+        @pl.when(b == 2)
+        def _():
+            for i in range(ups):
+                direct(1, i).wait_recv()
+                onward(1, i).start()
+            for d in range(DOWN):
+                down_piece(Y_X, d).wait_recv()
+                down_piece(D_P, d).start()
+
+        @pl.when(b == 3)
+        def _():
+            for d in range(DOWN):
+                down_piece(X_P, d).wait_recv()
+                down_piece(D_P, d).wait_recv()
+
+        @pl.loop(0, 2 * DOWN)
+        def _(p):
+            load_down(b, p)
+
+        @pl.loop(0, 2 * DOWN)
+        def _(p):
+            wait_down(p)
+
+            @pl.loop(0, ups)
+            def _(i):
+                down(b, p, i)
+
+                @pl.when(p == 2 * DOWN - 1)
+                def _():
+                    hand_out(b, i)
+
+    for b in (2, 3):
+        for i in range(ups):
+            direct(b, i).wait_recv()
+            onward(b, i).start()
     for g in range(blocks):
         drain(g, first(g), False)
 
     @pl.loop(0, groups)
     def _(b):
         drain(blocks + b, second(b), True)
+
+    for d in range(DOWN):
+        for kind in (OWN_X, OWN_Y, OWN_P, X_P, Y_P, Y_X, D_P):
+            down_piece(kind, d).wait_send()
 
     for q in range(NX):
         for p in (1, 2, 3):
@@ -512,19 +622,17 @@
             in_specs=[ANY, pl.BlockSpec(memory_space=pltpu.VMEM)] + [ANY] * 11,
             out_specs=[ANY] * 8,
             scratch_shapes=[pltpu.VMEM((rows, model), BF16), pltpu.VMEM((rows, model), F32),
-                            pltpu.VMEM((2, NDEV, width, LANES), BF16), pltpu.VMEM((2, NDEV, width, LANES), BF16),
-                            pltpu.VMEM((2, NDEV, LANES, width), BF16),
-                            pltpu.VMEM((total, LANES, LANES), BF16), pltpu.VMEM((total, LANES, LANES), BF16),
+                            pltpu.VMEM((NCH, rows, w_g.shape[1]), BF16), pltpu.VMEM((4, NDEV, width, LANES), BF16),
                             pltpu.VMEM((total, 16, LANES), F32), pltpu.VMEM((NCH, *vmlp.shape), F32), pltpu.VMEM((NWD, *vwd.shape), F32),
-                            pltpu.VMEM((CHUNK, model), BF16), pltpu.VMEM((2, 2, CHUNK, LANES), F32), pltpu.VMEM((CHUNK + 24, LANES), F32),
+                            pltpu.VMEM((2, 2, CHUNK, LANES), F32), pltpu.VMEM((CHUNK + 24, LANES), F32),
                             pltpu.VMEM((CHUNK, LANES), F32), pltpu.VMEM((CHUNK, LANES), F32), pltpu.VMEM((CHUNK, LANES), BF16),
-                            pltpu.VMEM((24, LANES), F32), pltpu.VMEM((8, LANES), F32), pltpu.VMEM((2, UP, NCH * LANES), BF16),
+                            pltpu.VMEM((24, LANES), F32), pltpu.VMEM((8, LANES), F32),
                             pltpu.VMEM((total, 32, LANES), F32), pltpu.VMEM((total, 32, LANES), F32),
-                            dma(kinds), dma(kinds), dma((2, 3, NDEV)), dma((3, NX)), dma((3, NX)), dma((7,)), dma((7,)), dma((5,)),
+                            dma(kinds), dma(kinds), dma((8, DOWN)), dma((8, DOWN)), dma((4, 3, NDEV)), dma((3, NX)), dma((3, NX)), dma((7,)), dma((7,)), dma((5,)),
                             dma((total,)), dma((total,)), dma((NWD,)), dma((3, ups)), dma((3, ups)), dma((4, ups)), dma((4, ups)), dma((ups,))],
             compiler_params=pltpu.CompilerParams(has_side_effects=True, vmem_limit_bytes=VMEM_LIMIT),
             name="layer",
-        )(resid_in, pos, w_y, w_x, w_o, w_g, w_u, w_d, rgate_w, igate_w, vch, vmlp, vwd)
+        )(resid_in, pos, w_y, w_x, w_o, w_g, w_u, w_d, rgate_w.reshape(-1, LANES), igate_w.reshape(-1, LANES), vch, vmlp, vwd)
         return outs[0]
 
     return jax.shard_map(local_layer, mesh=mesh, in_specs=specs, out_specs=row_spec, check_vma=False)

time: 813 us -> 741 us (0.911)
  Pallas kernels: 784 us -> 713 us
    pallas_call x1, Pallas kernels: 784 us -> 713 us  [local_layer(): pl.pallas_call(layer, out_shape=[jax.ShapeDtypeStruct((tokens, width), BF...]
where the time goes in v1:
time: 741 us; the launch traced here: 740 us
  Pallas kernels  713 us (96%)
  local copies, waits for them, and re-layouts  24.6 us (3%)
    pallas_call x1, Pallas kernels, local_layer(): pl.pallas_call(layer, out_shape=[jax.ShapeDtypeStruct((tokens, width), BF...  713 us

profile of v1, /device:TPU:0, one launch (start us, length us, event | category | flops | bytes accessed | tf_op | source)
XLA Modules:
  0.0 740.3 jit_solution(1078933033226183213)
XLA Ops:
  0.0 0.7 stack.79
  0.7 0.7 stack.80
  1.4 0.7 stack.81
  2.0 0.7 stack.82
  2.7 0.7 reshape.23
  3.4 0.7 reshape.24
  4.1 0.7 reshape.25
  4.8 0.7 reshape.26
  5.5 0.7 reshape.27
  6.2 0.6 fusion.11.vwd
  6.8 0.7 fusion.12
  7.5 0.7 stack.76
  8.2 0.7 stack.77
  8.9 0.9 slice_convert_fusion
  9.8 0.1 stack.75
  9.9 0.6 copy.29
  10.6 0.9 reshape.18
  11.5 0.1 reshape.19
  11.5 0.7 fusion.3.vmlp
  12.2 0.1 copy.25
  12.3 0.1 broadcast_in_dim.7
  12.4 1.3 broadcast_in_dim.8.pos_ref
  13.7 712.7 %layer.1 = (bf16[16384,512]{1,0:T(8,128)(2,1)}, bf16[8,512,1280]{2,1,0:T(8,128)(2,1)}, bf16[8,512,1280]{2,1,0:T(8,128)(2,1)}, bf16[8,1280,512]{2,1,0:T(8,128)(2,...) custom-call(bf16[16384,512]{1,0:T(8,128)(2,1)} %resid.1, ...), custom_call_target="tpu_custom_call" | custom-call | tf_op jit(solution)/shard_map/layer/pallas_call | solution.py:618
  726.5 13.8 %copy.31 = bf16[16384,512]{1,0:T(8,128)(2,1)} copy(bf16[16384,512]{1,0:T(8,128)(2,1)} %get-tuple-element.6) | data formatting | bytes 33554432
  (3 shorter events, 0.0 us)
